TPU v7x, 16 devices: a whole 2x2x2 slice. The times are simulated.
16 devices in a mesh: dp: 2 (over z), sp: 8 (over y, x, core).
Axes of the slice: x: 2, y: 2, z: 2, core: 2. Of those that a mesh axis runs over, the one named last changes fastest.
Arguments:
- x: bfloat16 [8192, 3072], P(('dp', 'sp')), parts along dimension 0
- grad_out: bfloat16 [8192, 3072], P(('dp', 'sp')), parts along dimension 0
- positions: int32 [8192], P(('dp', 'sp')), parts along dimension 0
- gain: bfloat16 [3072], replicated
- w_q: bfloat16 [3072, 3072], replicated
- w_k: bfloat16 [3072, 1024], replicated
- w_v: bfloat16 [3072, 1024], replicated
- w_o: bfloat16 [3072, 3072], replicated
Outputs:
- output 1: bfloat16 [8192, 3072], P(('dp', 'sp')), parts along dimension 0
- output 2: bfloat16 [8192, 3072], P(('dp', 'sp')), parts along dimension 0
- output 3: float32 [6144, 3072], P('dp'), parts along dimension 0
- output 4: float32 [6144, 1024], P('dp'), parts along dimension 0
- output 5: float32 [6144, 1024], P('dp'), parts along dimension 0
- output 6: float32 [6144, 3072], P('dp'), parts along dimension 0
- output 7: float32 [6144], P('dp'), parts along dimension 0
There are 2 independent parts. A program takes and returns all parts, laid end to end along the dimension named above; an argument that names none is the same for every part.
All inputs are finite; a program needn't handle non-finite values.
Results may differ from a plain program's by a relative error of at most 0.0182909.
Values are sent between devices in bfloat16 or wider.
A program may use at most 1 GiB of HBM per device.

v0:
```python
import jax
import jax.numpy as jnp
from jax import lax
from jax.sharding import PartitionSpec as P

HEAD_DIM = 128
ROPE_THETA = 1000000.0
NORM_EPS = 1e-05
NEG_LARGE = -1e30
CONTRACT_ROWS = (((0,), (0,)), ((), ()))
CONTRACT_COLS = (((1,), (1,)), ((), ()))


def block_rows(seq_len, row_cost):
    row_count = seq_len
    while row_count > 8 and row_count * row_cost > 2 ** 24:
        row_count = row_count // 2
    return row_count


def rope_tables(positions):
    inv_freq = ROPE_THETA ** (-jnp.arange(0, HEAD_DIM, 2).astype(jnp.float32) / HEAD_DIM)
    angles = positions.astype(jnp.float32)[:, None] * inv_freq[None, :]
    return jnp.cos(angles)[:, None, :], jnp.sin(angles)[:, None, :]


def rotate(values, cos_t, sin_t):
    half_dim = values.shape[-1] // 2
    lower_half = values[..., :half_dim]
    upper_half = values[..., half_dim:]
    return jnp.concatenate([lower_half * cos_t - upper_half * sin_t, upper_half * cos_t + lower_half * sin_t], axis=-1)


def attn_forward(q_all, k_all, v_all):
    seq_len, kv_loc, group_size, head_dim = q_all.shape
    row_count = block_rows(seq_len, kv_loc * group_size * seq_len)
    n_blocks = seq_len // row_count
    qk_scale = head_dim ** -0.5
    key_index = jnp.arange(seq_len)
    q_blocks = q_all.reshape(n_blocks, row_count, kv_loc, group_size, head_dim)
    blk_starts = jnp.arange(n_blocks) * row_count

    def one_block(block_args):
        q_blk, blk_start = block_args
        scores = jnp.einsum('qhgd,khd->hgqk', q_blk, k_all, preferred_element_type=jnp.float32) * qk_scale
        causal = (blk_start + jnp.arange(row_count))[:, None] >= key_index[None, :]
        attn_prob = jax.nn.softmax(jnp.where(causal, scores, NEG_LARGE), axis=-1)
        blk_out = jnp.einsum('hgqk,khd->qhgd', attn_prob.astype(jnp.bfloat16), v_all, preferred_element_type=jnp.float32)
        return blk_out.astype(jnp.bfloat16)

    return lax.map(one_block, (q_blocks, blk_starts)).reshape(seq_len, kv_loc, group_size, head_dim)


def attn_backward(q_all, k_all, v_all, do_all):
    seq_len, kv_loc, group_size, head_dim = q_all.shape
    row_count = block_rows(seq_len, kv_loc * group_size * seq_len)
    n_blocks = seq_len // row_count
    qk_scale = head_dim ** -0.5
    key_index = jnp.arange(seq_len)
    q_blocks = q_all.reshape(n_blocks, row_count, kv_loc, group_size, head_dim)
    do_blocks = do_all.reshape(n_blocks, row_count, kv_loc, group_size, head_dim)
    blk_starts = jnp.arange(n_blocks) * row_count

    def one_block(acc_pair, block_args):
        dk_acc, dv_acc = acc_pair
        q_blk, do_blk, blk_start = block_args
        scores = jnp.einsum('qhgd,khd->hgqk', q_blk, k_all, preferred_element_type=jnp.float32) * qk_scale
        causal = (blk_start + jnp.arange(row_count))[:, None] >= key_index[None, :]
        attn_prob = jax.nn.softmax(jnp.where(causal, scores, NEG_LARGE), axis=-1)
        prob_bf = attn_prob.astype(jnp.bfloat16)
        dv_acc = dv_acc + jnp.einsum('hgqk,qhgd->khd', prob_bf, do_blk, preferred_element_type=jnp.float32)
        d_prob = jnp.einsum('qhgd,khd->hgqk', do_blk, v_all, preferred_element_type=jnp.float32)
        d_score = attn_prob * (d_prob - jnp.sum(attn_prob * d_prob, axis=-1, keepdims=True)) * qk_scale
        ds_bf = d_score.astype(jnp.bfloat16)
        dq_blk = jnp.einsum('hgqk,khd->qhgd', ds_bf, k_all, preferred_element_type=jnp.float32)
        dk_acc = dk_acc + jnp.einsum('hgqk,qhgd->khd', ds_bf, q_blk, preferred_element_type=jnp.float32)
        return (dk_acc, dv_acc), dq_blk.astype(jnp.bfloat16)

    zero_acc = jnp.zeros((seq_len, kv_loc, head_dim), jnp.float32)
    (dk_all, dv_all), dq_blocks = lax.scan(one_block, (zero_acc, zero_acc), (q_blocks, do_blocks, blk_starts))
    return dq_blocks.reshape(seq_len, kv_loc, group_size, head_dim), dk_all, dv_all


def solution(mesh):
    sp_size = mesh.shape['sp']
    seq_spec = P(('dp', 'sp'), None)
    pos_spec = P(('dp', 'sp'))
    replicated = P(None, None)
    part_rows = P('dp', None)

    def local_step(x, grad_out, positions, gain, w_q, w_k, w_v, w_o):
        tok_count = x.shape[0]
        n_heads = w_q.shape[1] // HEAD_DIM
        kv_heads = w_k.shape[1] // HEAD_DIM
        kv_copies = max(1, sp_size // kv_heads)
        q_loc = n_heads // sp_size
        kv_loc = max(kv_heads, sp_size) // sp_size
        group_size = q_loc // kv_loc
        seq_len = tok_count * sp_size
        x_f = x.astype(jnp.float32)
        inv_rms = lax.rsqrt(jnp.mean(x_f * x_f, axis=-1, keepdims=True) + NORM_EPS)
        normed = x_f * inv_rms
        gain_f = gain.astype(jnp.float32)
        hidden = (normed * gain_f).astype(jnp.bfloat16)
        cos_t, sin_t = rope_tables(positions)
        q_proj = jnp.dot(hidden, w_q, preferred_element_type=jnp.float32).reshape(tok_count, n_heads, HEAD_DIM)
        k_proj = jnp.dot(hidden, w_k, preferred_element_type=jnp.float32).reshape(tok_count, kv_heads, HEAD_DIM)
        v_send = jnp.dot(hidden, w_v, preferred_element_type=jnp.float32).astype(jnp.bfloat16).reshape(tok_count, kv_heads, HEAD_DIM)
        q_rot = rotate(q_proj, cos_t, sin_t).astype(jnp.bfloat16)
        k_send = rotate(k_proj, cos_t, sin_t).astype(jnp.bfloat16)
        if kv_copies > 1:
            k_send = jnp.repeat(k_send, kv_copies, axis=1)
            v_send = jnp.repeat(v_send, kv_copies, axis=1)
        q_all = lax.all_to_all(q_rot, 'sp', 1, 0, tiled=True).reshape(seq_len, kv_loc, group_size, HEAD_DIM)
        k_all = lax.all_to_all(k_send, 'sp', 1, 0, tiled=True)
        v_all = lax.all_to_all(v_send, 'sp', 1, 0, tiled=True)
        o_all = attn_forward(q_all, k_all, v_all)
        o_loc = lax.all_to_all(o_all.reshape(seq_len, q_loc, HEAD_DIM), 'sp', 0, 1, tiled=True).reshape(tok_count, n_heads * HEAD_DIM)
        mixed = jnp.dot(o_loc, w_o, preferred_element_type=jnp.float32)
        result = (x_f + mixed).astype(jnp.bfloat16)
        grad_wo = lax.psum(lax.dot_general(o_loc, grad_out, CONTRACT_ROWS, preferred_element_type=jnp.float32), 'sp')
        d_o = lax.dot_general(grad_out, w_o, CONTRACT_COLS, preferred_element_type=jnp.float32).astype(jnp.bfloat16)
        do_all = lax.all_to_all(d_o.reshape(tok_count, n_heads, HEAD_DIM), 'sp', 1, 0, tiled=True).reshape(seq_len, kv_loc, group_size, HEAD_DIM)
        dq_all, dk_all, dv_all = attn_backward(q_all, k_all, v_all, do_all)
        dq_loc = lax.all_to_all(dq_all.reshape(seq_len, q_loc, HEAD_DIM), 'sp', 0, 1, tiled=True)
        dk_loc = lax.all_to_all(dk_all.astype(jnp.bfloat16), 'sp', 0, 1, tiled=True)
        dv_loc = lax.all_to_all(dv_all.astype(jnp.bfloat16), 'sp', 0, 1, tiled=True)
        dk_sum = jnp.sum(dk_loc.reshape(tok_count, kv_heads, kv_copies, HEAD_DIM), axis=2, dtype=jnp.float32)
        dv_sum = jnp.sum(dv_loc.reshape(tok_count, kv_heads, kv_copies, HEAD_DIM), axis=2, dtype=jnp.float32)
        dq_pre = rotate(dq_loc.astype(jnp.float32), cos_t, -sin_t).astype(jnp.bfloat16).reshape(tok_count, n_heads * HEAD_DIM)
        dk_pre = rotate(dk_sum, cos_t, -sin_t).astype(jnp.bfloat16).reshape(tok_count, kv_heads * HEAD_DIM)
        dv_pre = dv_sum.astype(jnp.bfloat16).reshape(tok_count, kv_heads * HEAD_DIM)
        grad_wq = lax.psum(lax.dot_general(hidden, dq_pre, CONTRACT_ROWS, preferred_element_type=jnp.float32), 'sp')
        grad_wk = lax.psum(lax.dot_general(hidden, dk_pre, CONTRACT_ROWS, preferred_element_type=jnp.float32), 'sp')
        grad_wv = lax.psum(lax.dot_general(hidden, dv_pre, CONTRACT_ROWS, preferred_element_type=jnp.float32), 'sp')
        d_hidden = (lax.dot_general(dq_pre, w_q, CONTRACT_COLS, preferred_element_type=jnp.float32)
                    + lax.dot_general(dk_pre, w_k, CONTRACT_COLS, preferred_element_type=jnp.float32)
                    + lax.dot_general(dv_pre, w_v, CONTRACT_COLS, preferred_element_type=jnp.float32))
        grad_gain = lax.psum(jnp.sum(d_hidden * normed, axis=0), 'sp')
        d_normed = d_hidden * gain_f
        d_xnorm = inv_rms * (d_normed - normed * jnp.mean(d_normed * normed, axis=-1, keepdims=True))
        grad_x = (grad_out.astype(jnp.float32) + d_xnorm).astype(jnp.bfloat16)
        return result, grad_x, grad_wq, grad_wk, grad_wv, grad_wo, grad_gain

    return jax.shard_map(local_step, mesh=mesh,
                         in_specs=(seq_spec, seq_spec, pos_spec, P(None), replicated, replicated, replicated, replicated),
                         out_specs=(seq_spec, seq_spec, part_rows, part_rows, part_rows, part_rows, P('dp')),
                         check_vma=False)
```

profile of v0, /device:TPU:0, one launch (start us, length us, event | category | flops | bytes accessed | tf_op | source)
XLA Modules:
  0.0 2556.5 jit_solution(15856317680537856531)
XLA Ops:
  24.4 13.8 fusion.78
  97.4 27.6 %all-to-all-done = bf16[512,24,128]{2,0,1:T(8,128)(2,1)S(1)} async-done(((bf16[512,24,128]{2,0,1:T(8,128)(2,1)}), bf16[512,24,128]{2,0,1:T(8,128)(2,1)S(1)}, u32[]{:S(2)}, u32[]{:S(2)}) %all-to-all-start) | async-done | bytes 3145760 | tf_op jit(solution)/shard_map/all_to_all | solution.py:114
  146.8 713.6 %while.27 = (s32[]{:T(128)}, f32[4096,1,128]{0,2,1:T(8,128)}, f32[4096,1,128]{0,2,1:T(8,128)}, bf16[4,1024,1,3,128]{4,1,0,3,2:T(8,128)(2,1)}, bf16[4,1024,1,3,12...) while((s32[]{:T(128)}, f32[4096,1,128]{0,2,1:T(8,128)}, ...), condition=%wide.region_9.10_spmd.clone, body=%wide.region_5.9_spmd.clone.sunk | while | flops 16439959552 | bytes 502149344 | solution.py:80
  151.9 23.2 fusion.144
  175.1 23.5 fusion.145
  198.6 24.0 fusion.149
  222.7 36.6 %fusion.146 = (f32[3,1024]{1,0:T(4,128)S(1)}, f32[1024,3,4096]{2,0,1:T(8,128)}) fusion(f32[3,1024]{1,0:T(4,128)S(1)} %fusion.145, f32[3,1024]{1,0:T(4,128)S(1)} %get-tuple-element.382, f32[1024,3,4096]{2,0,1:T(8,128)} %get-tuple-element.381, pred[1024,4096]{1,0:T(8,128)(4,1)} %copy-done, bf16[4096,1,128]{2,0,1:T(8,128)(2,1)} %get-tuple-element.436, ...), kind=kOutput, calls=%fused_computation.25.clone.1 | convolution fusion | flops 3296719872 | bytes 106729472 | tf_op jit(solution)/shard_map/while/body/eval_jaxpr/qhgd,khd->hgqk/dot_general | solution.py:72
  259.3 41.7 %fusion.147 = bf16[3,1024,4096]{2,1,0:T(8,128)(2,1)} fusion(f32[1024,3,4096]{2,0,1:T(8,128)} %get-tuple-element.383, f32[3,1024]{1,0:T(4,128)S(1)} %get-tuple-element.384, f32[3,1024]{1,0:T(4,128)S(1)} %fusion.145, f32[3,1024]{1,0:T(4,128)S(1)} %get-tuple-element.382, f32[1024,3,4096]{2,0,1:T(8,128)} %get-tuple-element.381, pred[1024,4096]{1,0:T(8,128)(4,1)} %copy-done), kind=kLoop, calls=%fused_computation.33.clone.1 | loop fusion | flops 100663296 | bytes 130060288 | tf_op jit(solution)/shard_map/reshape.35
  311.3 13.4 fusion.150
  329.6 23.2 fusion.144
  352.9 23.5 fusion.145
  376.4 24.7 fusion.149
  401.1 36.6 %fusion.146 = (f32[3,1024]{1,0:T(4,128)S(1)}, f32[1024,3,4096]{2,0,1:T(8,128)}) fusion(f32[3,1024]{1,0:T(4,128)S(1)} %fusion.145, f32[3,1024]{1,0:T(4,128)S(1)} %get-tuple-element.382, f32[1024,3,4096]{2,0,1:T(8,128)} %get-tuple-element.381, pred[1024,4096]{1,0:T(8,128)(4,1)} %copy-done, bf16[4096,1,128]{2,0,1:T(8,128)(2,1)} %get-tuple-element.436, ...), kind=kOutput, calls=%fused_computation.25.clone.1 | convolution fusion | flops 3296719872 | bytes 106729472 | tf_op jit(solution)/shard_map/while/body/eval_jaxpr/qhgd,khd->hgqk/dot_general | solution.py:72
  437.7 41.7 %fusion.147 = bf16[3,1024,4096]{2,1,0:T(8,128)(2,1)} fusion(f32[1024,3,4096]{2,0,1:T(8,128)} %get-tuple-element.383, f32[3,1024]{1,0:T(4,128)S(1)} %get-tuple-element.384, f32[3,1024]{1,0:T(4,128)S(1)} %fusion.145, f32[3,1024]{1,0:T(4,128)S(1)} %get-tuple-element.382, f32[1024,3,4096]{2,0,1:T(8,128)} %get-tuple-element.381, pred[1024,4096]{1,0:T(8,128)(4,1)} %copy-done), kind=kLoop, calls=%fused_computation.33.clone.1 | loop fusion | flops 100663296 | bytes 130060288 | tf_op jit(solution)/shard_map/reshape.35
  508.0 23.2 fusion.144
  531.3 23.5 fusion.145
  554.8 24.7 fusion.149
  579.5 36.6 %fusion.146 = (f32[3,1024]{1,0:T(4,128)S(1)}, f32[1024,3,4096]{2,0,1:T(8,128)}) fusion(f32[3,1024]{1,0:T(4,128)S(1)} %fusion.145, f32[3,1024]{1,0:T(4,128)S(1)} %get-tuple-element.382, f32[1024,3,4096]{2,0,1:T(8,128)} %get-tuple-element.381, pred[1024,4096]{1,0:T(8,128)(4,1)} %copy-done, bf16[4096,1,128]{2,0,1:T(8,128)(2,1)} %get-tuple-element.436, ...), kind=kOutput, calls=%fused_computation.25.clone.1 | convolution fusion | flops 3296719872 | bytes 106729472 | tf_op jit(solution)/shard_map/while/body/eval_jaxpr/qhgd,khd->hgqk/dot_general | solution.py:72
  616.1 41.7 %fusion.147 = bf16[3,1024,4096]{2,1,0:T(8,128)(2,1)} fusion(f32[1024,3,4096]{2,0,1:T(8,128)} %get-tuple-element.383, f32[3,1024]{1,0:T(4,128)S(1)} %get-tuple-element.384, f32[3,1024]{1,0:T(4,128)S(1)} %fusion.145, f32[3,1024]{1,0:T(4,128)S(1)} %get-tuple-element.382, f32[1024,3,4096]{2,0,1:T(8,128)} %get-tuple-element.381, pred[1024,4096]{1,0:T(8,128)(4,1)} %copy-done), kind=kLoop, calls=%fused_computation.33.clone.1 | loop fusion | flops 100663296 | bytes 130060288 | tf_op jit(solution)/shard_map/reshape.35
  686.4 23.2 fusion.144
  709.7 23.5 fusion.145
  733.2 24.7 fusion.149
  757.9 36.6 %fusion.146 = (f32[3,1024]{1,0:T(4,128)S(1)}, f32[1024,3,4096]{2,0,1:T(8,128)}) fusion(f32[3,1024]{1,0:T(4,128)S(1)} %fusion.145, f32[3,1024]{1,0:T(4,128)S(1)} %get-tuple-element.382, f32[1024,3,4096]{2,0,1:T(8,128)} %get-tuple-element.381, pred[1024,4096]{1,0:T(8,128)(4,1)} %copy-done, bf16[4096,1,128]{2,0,1:T(8,128)(2,1)} %get-tuple-element.436, ...), kind=kOutput, calls=%fused_computation.25.clone.1 | convolution fusion | flops 3296719872 | bytes 106729472 | tf_op jit(solution)/shard_map/while/body/eval_jaxpr/qhgd,khd->hgqk/dot_general | solution.py:72
  794.6 41.7 %fusion.147 = bf16[3,1024,4096]{2,1,0:T(8,128)(2,1)} fusion(f32[1024,3,4096]{2,0,1:T(8,128)} %get-tuple-element.383, f32[3,1024]{1,0:T(4,128)S(1)} %get-tuple-element.384, f32[3,1024]{1,0:T(4,128)S(1)} %fusion.145, f32[3,1024]{1,0:T(4,128)S(1)} %get-tuple-element.382, f32[1024,3,4096]{2,0,1:T(8,128)} %get-tuple-element.381, pred[1024,4096]{1,0:T(8,128)(4,1)} %copy-done), kind=kLoop, calls=%fused_computation.33.clone.1 | loop fusion | flops 100663296 | bytes 130060288 | tf_op jit(solution)/shard_map/reshape.35
  846.6 13.4 fusion.150
  890.4 299.9 %while.26 = (s32[]{:T(128)}, bf16[4,1024,1,3,128]{4,1,0,3,2:T(8,128)(2,1)S(1)}, s32[4]{0:T(128)}, bf16[4,1024,1,3,128]{4,1,3,2,0:T(8,128)(2,1)}, bf16[4096,1,128...) while((s32[]{:T(128)}, bf16[4,1024,1,3,128]{4,1,0,3,2:T(8,128)(2,1)S(1)}, ...), condition=%wide.region_4.5_spmd.clone, body=%wide.region_1.4_spmd.clone.sunk | while | flops 6598028288 | bytes 188297360 | solution.py:51
  895.5 23.2 fusion.135
  918.8 23.5 fusion.136
  942.3 23.1 fusion.137
  970.4 23.2 fusion.135
  993.6 23.5 fusion.136
  1017.1 23.1 fusion.137
  1045.2 23.2 fusion.135
  1068.4 23.5 fusion.136
  1091.9 23.1 fusion.137
  1120.0 23.2 fusion.135
  1143.3 23.5 fusion.136
  1166.8 23.1 fusion.137
  1203.5 20.4 copy.127
  1223.9 28.5 %all-to-all-done.3 = bf16[4096,3,128]{2,1,0:T(4,128)(2,1)} async-done(((bf16[4096,3,128]{2,1,0:T(4,128)(2,1)}), bf16[4096,3,128]{2,1,0:T(4,128)(2,1)}, u32[]{:S(2)}, u32[]{:S(2)}) %all-to-all-start.3) | async-done | bytes 3145760 | tf_op jit(solution)/shard_map/all_to_all | solution.py:118
  1317.2 21.1 fusion.85
  1338.2 16.4 fusion.94
  1372.8 17.9 fusion.75
  1390.7 23.3 psum.39
  1420.2 15.3 fusion.77
  1435.5 1033.9 %all-reduce.3.cloned.1.call-done = (f32[3072,3072]{1,0:T(8,128)}, f32[3072,1024]{1,0:T(8,128)}, f32[3072,1024]{1,0:T(8,128)}, f32[3072,3072]{1,0:T(8,128)}) async-done(((f32[3072,3072]{1,0:T(8,128)}, f32[3072,1024]{1,0:T(8,128)}, f32[3072,1024]{1,0:T(8,128)}, f32[3072,3072]{1,0:T(8,128)}), (f32[3072,3072]{1,0:T(8,128)}, f32[3072,1024]{1,0:T(8,128)}, f32[3072,1024]{1,0:T(8,128)}, ...) | async-done | bytes 100663312 | tf_op jit(solution)/shard_map/psum | solution.py:133
  2469.3 27.9 %copy.191 = f32[3072,3072]{1,0:T(8,128)} copy(f32[3072,3072]{1,0:T(8,128)} %get-tuple-element.441) | data formatting | bytes 75497472
  2521.4 27.9 %copy.194 = f32[3072,3072]{1,0:T(8,128)} copy(f32[3072,3072]{1,0:T(8,128)} %get-tuple-element.444) | data formatting | bytes 75497472
  (190 shorter events, 361.1 us)
Async XLA Ops:
  9.8 77.5 %copy-start.26 = (f32[512]{0:T(512)}, f32[512]{0:T(512)S(1)}, u32[]{:S(2)}) copy-start(f32[512]{0:T(512)S(1)} %add_rsqrt_fusion) | copy-start | bytes 6148
  10.5 76.8 %copy-start.24 = (f32[3072]{0:T(1024)}, f32[3072]{0:T(1024)S(1)}, u32[]{:S(2)}) copy-start(f32[3072]{0:T(1024)S(1)} %convert_element_type.123) | copy-start | bytes 36868
  10.5 14.0 copy-start.16
  19.0 21.8 all-to-all-start.2
  38.3 7.2 copy-start.6
  40.8 42.4 %all-to-all-start.4 = ((bf16[512,24,128]{2,0,1:T(8,128)(2,1)}), bf16[512,24,128]{2,0,1:T(8,128)(2,1)}, u32[]{:S(2)}, u32[]{:S(2)}) async-start(bf16[512,24,128]{2,0,1:T(8,128)(2,1)} %bitcast.239), calls=%async_computation.4 | async-start | bytes 6291456 | tf_op jit(solution)/shard_map/all_to_all | solution.py:123
  45.5 13.2 copy-start.28
  61.9 33.1 %copy-start.9 = (f32[512,64]{1,0:T(8,128)}, f32[512,64]{1,0:T(8,128)S(1)}, u32[]{:S(2)}) copy-start(f32[512,64]{1,0:T(8,128)S(1)} %get-tuple-element.279) | copy-start | bytes 393220
  83.2 41.8 %all-to-all-start = ((bf16[512,24,128]{2,0,1:T(8,128)(2,1)}), bf16[512,24,128]{2,0,1:T(8,128)(2,1)S(1)}, u32[]{:S(2)}, u32[]{:S(2)}) async-start(bf16[512,24,128]{2,0,1:T(8,128)(2,1)} %pad_maximum_fusion), calls=%async_computation | async-start | bytes 6291456 | tf_op jit(solution)/shard_map/all_to_all | solution.py:114
  93.9 1.2 copy-start.20
  125.0 19.5 all-to-all-start.1
  151.8 23.3 copy-start
  259.3 41.7 %copy-start.2 = (f32[4096,1,128]{0,2,1:T(8,128)S(1)}, f32[4096,1,128]{0,2,1:T(8,128)}, u32[]{:S(2)}) copy-start(f32[4096,1,128]{0,2,1:T(8,128)} %get-tuple-element.418) | copy-start | bytes 6291460 | tf_op jit(solution)/shard_map/while
  311.3 13.4 copy-start.3
  329.6 23.3 copy-start
  437.7 41.7 %copy-start.2 = (f32[4096,1,128]{0,2,1:T(8,128)S(1)}, f32[4096,1,128]{0,2,1:T(8,128)}, u32[]{:S(2)}) copy-start(f32[4096,1,128]{0,2,1:T(8,128)} %get-tuple-element.418) | copy-start | bytes 6291460 | tf_op jit(solution)/shard_map/while
  489.7 13.4 copy-start.3
  508.0 23.3 copy-start
  616.1 41.7 %copy-start.2 = (f32[4096,1,128]{0,2,1:T(8,128)S(1)}, f32[4096,1,128]{0,2,1:T(8,128)}, u32[]{:S(2)}) copy-start(f32[4096,1,128]{0,2,1:T(8,128)} %get-tuple-element.418) | copy-start | bytes 6291460 | tf_op jit(solution)/shard_map/while
  668.1 13.4 copy-start.3
  686.4 23.3 copy-start
  794.6 41.7 %copy-start.2 = (f32[4096,1,128]{0,2,1:T(8,128)S(1)}, f32[4096,1,128]{0,2,1:T(8,128)}, u32[]{:S(2)}) copy-start(f32[4096,1,128]{0,2,1:T(8,128)} %get-tuple-element.418) | copy-start | bytes 6291460 | tf_op jit(solution)/shard_map/while
  846.6 13.4 copy-start.3
  865.8 18.9 all-to-all-start.6
  884.6 1.0 copy-start.11
  885.6 313.2 %all-to-all-start.7 = ((bf16[8,2,32768]{2,1,0:T(2,128)(2,1)}), bf16[8,2,32768]{2,1,0:T(2,128)(2,1)}, u32[]{:S(2)}, u32[]{:S(2)}) async-start(bf16[8,2,32768]{2,1,0:T(2,128)(2,1)} %reshape.260), calls=%async_computation.7 | async-start | bytes 2097152 | tf_op jit(solution)/shard_map/all_to_all | solution.py:127
  895.5 23.3 copy-start.1
  970.4 23.3 copy-start.1
  1045.2 23.3 copy-start.1
  1120.0 23.3 copy-start.1
  1190.3 1.7 copy-start.5
  1192.0 11.5 copy-start.4
  1198.9 53.6 %all-to-all-start.3 = ((bf16[4096,3,128]{2,1,0:T(4,128)(2,1)}), bf16[4096,3,128]{2,1,0:T(4,128)(2,1)}, u32[]{:S(2)}, u32[]{:S(2)}) async-start(bf16[4096,3,128]{2,1,0:T(4,128)(2,1)} %copy.119), calls=%async_computation.3 | async-start | bytes 8388608 | tf_op jit(solution)/shard_map/all_to_all | solution.py:118
  1223.9 33.2 %copy-start.12 = (bf16[8,2,32768]{2,1,0:T(2,128)(2,1)S(1)}, bf16[8,2,32768]{2,1,0:T(2,128)(2,1)}, u32[]{:S(2)}) copy-start(bf16[8,2,32768]{2,1,0:T(2,128)(2,1)} %copy-done.11) | copy-start | bytes 3145732
  1252.4 53.6 %all-to-all-start.5 = ((bf16[4096,3,128]{2,1,0:T(4,128)(2,1)}), bf16[4096,3,128]{2,1,0:T(4,128)(2,1)}, u32[]{:S(2)}, u32[]{:S(2)}) async-start(bf16[4096,3,128]{2,1,0:T(4,128)(2,1)} %copy.127), calls=%async_computation.5 | async-start | bytes 8388608 | tf_op jit(solution)/shard_map/all_to_all | solution.py:125
  1257.0 1.4 copy-start.10
  1257.0 1212.3 %all-reduce.3.cloned.1.call-start = ((), (), s32[]{:S(2)}) async-start(), calls=%async_computation.8 | async-start | bytes 201326592 | tf_op jit(solution)/shard_map/psum | solution.py:133
  1259.9 14.6 copy-start.7
  1259.9 14.6 copy-start.25
  1259.9 14.6 copy-start.27
  1274.4 8.1 copy-start.22
  1317.2 21.1 copy-start.13
  1317.2 21.1 copy-start.17
  1354.7 1.2 copy-start.23
  1355.9 8.3 copy-start.21
  1364.2 8.6 copy-start.8
  1364.2 8.6 copy-start.15
  1414.0 6.2 copy-start.14
  (2 other events, 1.9 us)
Sparse Core Ops, SparseCore 0:
  1354.8 1114.4 all-reduce.2
where the time goes:
time: 2570 us; the launch traced here: 2560 us
  waiting for transfers between devices  1120 us (44%)
  matrix products  761 us (30%)
  other arithmetic  423 us (16%)
  local copies, waits for them, and re-layouts  174 us (7%)
  starting transfers between devices  35.4 us (1%)
    psum x1, waiting for transfers between devices, local_step(): lax.psum(lax.dot_general(hidden, dq_pre, CONTRACT_ROWS, preferred_element...  1030 us
    reduce_sum x8, other arithmetic, one_block(): attn_prob = jax.nn.softmax(jnp.where(causal, scores, NEG_LARGE), axis=-1)  188 us
    dot_general x8, matrix products, one_block(): jnp.einsum('qhgd,khd->hgqk', q_blk, k_all, preferred_element_type=jnp.flo...  186 us
    another operation x8, other arithmetic  179 us
    dot_general x4, matrix products, one_block(): jnp.einsum('qhgd,khd->hgqk', do_blk, v_all, preferred_element_type=jnp.fl...  147 us
    unnamed x64, local copies, waits for them, and re-layouts  102 us
    dot_general x4, matrix products, one_block(): jnp.einsum('hgqk,qhgd->khd', prob_bf, do_blk, preferred_element_type=jnp....  98.2 us
    dot_general x4, matrix products, one_block(): jnp.einsum('hgqk,khd->qhgd', attn_prob.astype(jnp.bfloat16), v_all, prefe...  92.4 us
  transfers between devices with their start and end apart: 9, of which 7 were waited for; matrix products, arithmetic and copies ran while one was open for 19% of the time, Pallas kernels for 0%

commit v1 on v0

v1 whole, which is shorter than its diff:
```python
import functools

import jax
import jax.numpy as jnp
from jax import lax
from jax.experimental import pallas as pl
from jax.experimental.pallas import tpu as pltpu
from jax.sharding import PartitionSpec as P


HEAD_DIM = 128
HALF = HEAD_DIM // 2
ROPE_THETA = 1000000.0
NORM_EPS = 1e-05
NEG_LARGE = -1e30
LOG2E = 1.4426950408889634
BLK = 512
F32 = jnp.float32
BF16 = jnp.bfloat16
ROWS_ROWS = (((0,), (0,)), ((), ()))
COLS_COLS = (((1,), (1,)), ((), ()))
ROWS_COLS = (((0,), (1,)), ((), ()))
VMEM_LIMIT = 60 * 1024 * 1024


def dot(a, b, dims=(((1,), (0,)), ((), ()))):
    return lax.dot_general(a, b, dims, preferred_element_type=F32)


def params():
    return pltpu.CompilerParams(dimension_semantics=("arbitrary",), vmem_limit_bytes=VMEM_LIMIT)


def rope_tables(positions):
    inv_freq = ROPE_THETA ** (-jnp.arange(0, HEAD_DIM, 2).astype(F32) / HEAD_DIM)
    angles = positions.astype(F32)[:, None] * inv_freq[None, :]
    return jnp.cos(angles), jnp.sin(angles)


def project_kernel(heads, h_ref, w_ref, cos_ref, sin_ref, q_ref, k_ref, v_ref):
    prod = dot(h_ref[...], w_ref[...])
    cos_t, sin_t = cos_ref[...], sin_ref[...]
    for i in range(heads + 1):
        val = prod[:, i * HEAD_DIM:(i + 1) * HEAD_DIM]
        rot = (val * cos_t + pltpu.roll(val, HALF, 1) * sin_t).astype(BF16)
        if i < heads:
            q_ref[:, i * HEAD_DIM:(i + 1) * HEAD_DIM] = rot
        else:
            k_ref[...] = rot
    v_ref[...] = prod[:, (heads + 1) * HEAD_DIM:].astype(BF16)


def project(hidden, w_all, cos_t, sin_t, heads):
    seq_len, width = hidden.shape
    rows = lambda i: (i, 0)
    q_cols = heads * HEAD_DIM
    return pl.pallas_call(
        functools.partial(project_kernel, heads),
        grid=(seq_len // BLK,),
        in_specs=[pl.BlockSpec((BLK, width), rows), pl.BlockSpec(w_all.shape, lambda i: (0, 0)),
                  pl.BlockSpec((BLK, HEAD_DIM), rows), pl.BlockSpec((BLK, HEAD_DIM), rows)],
        out_specs=[pl.BlockSpec((BLK, q_cols), rows), pl.BlockSpec((BLK, HEAD_DIM), rows), pl.BlockSpec((BLK, HEAD_DIM), rows)],
        out_shape=[jax.ShapeDtypeStruct((seq_len, q_cols), BF16), jax.ShapeDtypeStruct((seq_len, HEAD_DIM), BF16),
                   jax.ShapeDtypeStruct((seq_len, HEAD_DIM), BF16)],
        compiler_params=params(),
        cost_estimate=pl.CostEstimate(flops=2 * seq_len * width * w_all.shape[1], bytes_accessed=2 * seq_len * width, transcendentals=0),
        name="project",
    )(hidden, w_all, cos_t, sin_t)


def masked(scores):
    key = lax.broadcasted_iota(jnp.int32, scores.shape, 0)
    query = lax.broadcasted_iota(jnp.int32, scores.shape, 1)
    return jnp.where(key <= query, scores, NEG_LARGE)


def attn_fwd_kernel(heads, q_ref, k_ref, v_ref, o_ref, lse_ref, vt, acc):
    i = pl.program_id(0)
    n_blocks = k_ref.shape[0] // BLK
    to_log2 = HEAD_DIM ** -0.5 * LOG2E

    @pl.when(i == 0)
    def _():
        @pl.loop(0, n_blocks)
        def _(c):
            vt[c] = v_ref[pl.ds(c * BLK, BLK), :].T

    acc[...] = jnp.zeros_like(acc)

    def chunk(c, carry, diagonal):
        k_c = k_ref[pl.ds(pl.multiple_of(c * BLK, BLK), BLK), :]
        vt_c = vt[c]
        scores = [dot(k_c, q_ref[:, a * HEAD_DIM:(a + 1) * HEAD_DIM], COLS_COLS) * to_log2 for a in range(heads)]
        out = []
        for a in range(heads):
            s = masked(scores[a]) if diagonal else scores[a]
            m_old, l_old = carry[a]
            m_new = jnp.maximum(m_old, jnp.max(s, axis=0, keepdims=True))
            alpha = jnp.exp2(m_old - m_new)
            p = jnp.exp2(s - m_new)
            l_new = l_old * alpha + jnp.sum(p, axis=0, keepdims=True)
            acc[a] = acc[a] * alpha + dot(vt_c, p.astype(BF16))
            out.append((m_new, l_new))
        return tuple(out)

    start = tuple((jnp.full((1, BLK), NEG_LARGE, F32), jnp.zeros((1, BLK), F32)) for _ in range(heads))
    carry = lax.fori_loop(0, i, lambda c, carry: chunk(c, carry, False), start)
    carry = chunk(i, carry, True)
    for a in range(heads):
        m_a, l_a = carry[a]
        o_ref[a * HEAD_DIM:(a + 1) * HEAD_DIM, :] = (acc[a] / l_a).astype(BF16)
        lse_ref[a:a + 1, :] = m_a + jnp.log2(l_a)


def attn_forward(q, k, v, heads):
    seq_len = k.shape[0]
    n_blocks = seq_len // BLK
    whole = lambda i: (0, 0)
    pairs = heads * seq_len * (seq_len + BLK) // 2
    return pl.pallas_call(
        functools.partial(attn_fwd_kernel, heads),
        grid=(n_blocks,),
        in_specs=[pl.BlockSpec((BLK, heads * HEAD_DIM), lambda i: (i, 0)), pl.BlockSpec(k.shape, whole), pl.BlockSpec(v.shape, whole)],
        out_specs=[pl.BlockSpec((heads * HEAD_DIM, BLK), lambda i: (0, i)), pl.BlockSpec((8, BLK), lambda i: (0, i))],
        out_shape=[jax.ShapeDtypeStruct((heads * HEAD_DIM, seq_len), BF16), jax.ShapeDtypeStruct((8, seq_len), F32)],
        scratch_shapes=[pltpu.VMEM((n_blocks, HEAD_DIM, BLK), BF16), pltpu.VMEM((heads, HEAD_DIM, BLK), F32)],
        compiler_params=params(),
        cost_estimate=pl.CostEstimate(flops=8 * pairs * HEAD_DIM, bytes_accessed=4 * seq_len * heads * HEAD_DIM, transcendentals=pairs),
        name="attn_fwd",
    )(q, k, v)


def unrotate_t(val, cos_t, sin_t):
    lower, upper = val[:HALF], val[HALF:]
    return jnp.concatenate([lower * cos_t + upper * sin_t, upper * cos_t - lower * sin_t], axis=0)


def attn_bwd_kernel(heads, q_ref, k_ref, v_ref, do_ref, ot_ref, lse_ref, cos_ref, sin_ref, dq_ref, dk_ref, dv_ref, kt, dk_acc, dv_acc, dqt):
    i = pl.program_id(0)
    n_blocks = k_ref.shape[0] // BLK
    qk_scale = HEAD_DIM ** -0.5
    to_log2 = qk_scale * LOG2E

    @pl.when(i == 0)
    def _():
        @pl.loop(0, n_blocks)
        def _(c):
            kt[c] = k_ref[pl.ds(c * BLK, BLK), :].T

    dqt[...] = jnp.zeros_like(dqt)
    cols = [slice(a * HEAD_DIM, (a + 1) * HEAD_DIM) for a in range(heads)]
    delta = [jnp.sum(ot_ref[cols[a], :].astype(F32) * do_ref[:, cols[a]].T.astype(F32), axis=0, keepdims=True) for a in range(heads)]

    def chunk(c, diagonal):
        rows = pl.ds(pl.multiple_of(c * BLK, BLK), BLK)
        k_c, v_c, kt_c = k_ref[rows, :], v_ref[rows, :], kt[c]
        dk_c = dv_c = None
        for a in range(heads):
            q_a, do_a = q_ref[:, cols[a]], do_ref[:, cols[a]]
            s = dot(k_c, q_a, COLS_COLS) * to_log2
            if diagonal:
                s = masked(s)
            p = jnp.exp2(s - lse_ref[a:a + 1, :])
            d_p = dot(v_c, do_a, COLS_COLS)
            d_s = (p * (d_p - delta[a])).astype(BF16)
            dv_a = dot(p.astype(BF16), do_a)
            dk_a = dot(d_s, q_a)
            dv_c = dv_a if dv_c is None else dv_c + dv_a
            dk_c = dk_a if dk_c is None else dk_c + dk_a
            dqt[a] += dot(kt_c, d_s)
        if diagonal:
            dk_acc[c] = dk_c
            dv_acc[c] = dv_c
        else:
            dk_acc[c] += dk_c
            dv_acc[c] += dv_c

    @pl.loop(0, i)
    def _(c):
        chunk(c, False)

    chunk(i, True)
    for a in range(heads):
        dq_ref[cols[a], :] = unrotate_t(dqt[a] * qk_scale, cos_ref[i], sin_ref[i]).astype(BF16)

    @pl.when(i == n_blocks - 1)
    def _():
        for c in range(n_blocks):
            dk_ref[:, c * BLK:(c + 1) * BLK] = unrotate_t(dk_acc[c].T * qk_scale, cos_ref[c], sin_ref[c]).astype(BF16)
            dv_ref[:, c * BLK:(c + 1) * BLK] = dv_acc[c].astype(BF16).T


def attn_backward(q, k, v, d_o, ot, lse, cos_t, sin_t, heads):
    seq_len = k.shape[0]
    n_blocks = seq_len // BLK
    whole = lambda i: (0, 0)
    blocks = lambda t: t.T.reshape(HALF, n_blocks, BLK).transpose(1, 0, 2)
    pairs = heads * seq_len * (seq_len + BLK) // 2
    q_cols = heads * HEAD_DIM
    row_spec = pl.BlockSpec((BLK, q_cols), lambda i: (i, 0))
    col_spec = pl.BlockSpec((q_cols, BLK), lambda i: (0, i))
    table_spec = pl.BlockSpec((n_blocks, HALF, BLK), lambda i: (0, 0, 0))
    kv_spec = pl.BlockSpec(k.shape, whole)
    kvt_spec = pl.BlockSpec((HEAD_DIM, seq_len), whole)
    return pl.pallas_call(
        functools.partial(attn_bwd_kernel, heads),
        grid=(n_blocks,),
        in_specs=[row_spec, kv_spec, kv_spec, row_spec, col_spec, pl.BlockSpec((8, BLK), lambda i: (0, i)), table_spec, table_spec],
        out_specs=[col_spec, kvt_spec, kvt_spec],
        out_shape=[jax.ShapeDtypeStruct((q_cols, seq_len), BF16), jax.ShapeDtypeStruct((HEAD_DIM, seq_len), BF16),
                   jax.ShapeDtypeStruct((HEAD_DIM, seq_len), BF16)],
        scratch_shapes=[pltpu.VMEM((n_blocks, HEAD_DIM, BLK), BF16), pltpu.VMEM((n_blocks, BLK, HEAD_DIM), F32),
                        pltpu.VMEM((n_blocks, BLK, HEAD_DIM), F32), pltpu.VMEM((heads, HEAD_DIM, BLK), F32)],
        compiler_params=params(),
        cost_estimate=pl.CostEstimate(flops=20 * pairs * HEAD_DIM, bytes_accessed=8 * seq_len * q_cols, transcendentals=pairs),
        name="attn_bwd",
    )(q, k, v, d_o, ot, lse, blocks(cos_t), blocks(sin_t))


def solution(mesh):
    sp_size = mesh.shape['sp']
    seq_spec = P(('dp', 'sp'), None)
    pos_spec = P(('dp', 'sp'))
    replicated = P(None, None)
    part_rows = P('dp', None)

    def gather(val):
        return lax.all_gather(val, 'sp', axis=0, tiled=True)

    def local_step(x, grad_out, positions, gain, w_q, w_k, w_v, w_o):
        tok_count = x.shape[0]
        n_heads = w_q.shape[1] // HEAD_DIM
        heads = n_heads // sp_size
        me = lax.axis_index('sp')
        q_cols = heads * HEAD_DIM
        x_f = x.astype(F32)
        inv_rms = lax.rsqrt(jnp.mean(x_f * x_f, axis=-1, keepdims=True) + NORM_EPS)
        normed = x_f * inv_rms
        gain_f = gain.astype(F32)
        hidden = gather((normed * gain_f).astype(BF16))
        d_out = gather(grad_out)
        cos_h, sin_h = rope_tables(gather(positions))
        cos_t = jnp.concatenate([cos_h, cos_h], axis=1)
        sin_t = jnp.concatenate([-sin_h, sin_h], axis=1)
        take_cols = lambda w, n: lax.dynamic_slice_in_dim(w, me * n, n, axis=1)
        w_all = jnp.concatenate([take_cols(w_q, q_cols), take_cols(w_k, HEAD_DIM), take_cols(w_v, HEAD_DIM)], axis=1)
        w_o_loc = lax.dynamic_slice_in_dim(w_o, me * q_cols, q_cols, axis=0)

        q, k, v = project(hidden, w_all, cos_t, sin_t, heads)
        ot, lse = attn_forward(q, k, v, heads)
        ot_all = gather(ot)
        d_o = dot(d_out, w_o_loc, COLS_COLS).astype(BF16)
        dqt, dkt, dvt = attn_backward(q, k, v, d_o, ot, lse, cos_h, sin_h, heads)
        dqt_all, dkt_all, dvt_all = gather(dqt), gather(dkt), gather(dvt)

        own = lambda t: lax.dynamic_slice_in_dim(t, me * tok_count, tok_count, axis=1)
        result = (x_f + dot(own(ot_all), w_o, ROWS_ROWS)).astype(BF16)
        grad_wo = dot(ot_all, d_out)
        grad_wq = dot(hidden, dqt_all, ROWS_COLS)
        grad_wk = dot(hidden, dkt_all, ROWS_COLS)
        grad_wv = dot(hidden, dvt_all, ROWS_COLS)
        d_hidden = (dot(own(dqt_all), w_q, ROWS_COLS) + dot(own(dkt_all), w_k, ROWS_COLS) + dot(own(dvt_all), w_v, ROWS_COLS))
        grad_gain = lax.psum(jnp.sum(d_hidden * normed, axis=0), 'sp')
        d_normed = d_hidden * gain_f
        d_xnorm = inv_rms * (d_normed - normed * jnp.mean(d_normed * normed, axis=-1, keepdims=True))
        grad_x = (grad_out.astype(F32) + d_xnorm).astype(BF16)
        return result, grad_x, grad_wq, grad_wk, grad_wv, grad_wo, grad_gain

    return jax.shard_map(local_step, mesh=mesh,
                         in_specs=(seq_spec, seq_spec, pos_spec, P(None), replicated, replicated, replicated, replicated),
                         out_specs=(seq_spec, seq_spec, part_rows, part_rows, part_rows, part_rows, P('dp')),
                         check_vma=False)
```

time: 2570 us -> 930 us (0.36)
  waiting for transfers between devices: 1120 us -> 350 us
  matrix products: 761 us -> 320 us
  other arithmetic: 423 us -> 31.7 us
  local copies, waits for them, and re-layouts: 174 us -> 4.02 us
  Pallas kernels: 0 us -> 163 us
  starting transfers between devices: 35.4 us -> 0.64 us
    psum x1 -> x0, waiting for transfers between devices: 1030 us -> none  [local_step(): lax.psum(lax.dot_general(hidden, dq_pre, CONTRACT_ROWS, preferred_element...]
    dot_general x40 -> x9, matrix products: 761 us -> 320 us  [dot(): return lax.dot_general(a, b, dims, preferred_element_type=F32)]
    all_gather x0 -> x6, waiting for transfers between devices: none -> 348 us  [gather(): return lax.all_gather(val, 'sp', axis=0, tiled=True)]
    reduce_sum x9 -> x0, other arithmetic: 188 us -> none  [the longest x8 188 us: one_block(): attn_prob = jax.nn.softmax(jnp.where(causal, scores, NEG_LARGE), axis=-1)]
    another operation x8 -> x0, other arithmetic: 179 us -> none
    pallas_call x0 -> x3, Pallas kernels: none -> 163 us  [the longest x1 86.5 us: attn_backward(): pl.pallas_call(functools.partial(attn_bwd_kernel, heads), grid=(n_blocks,...]
    unnamed x64 -> x15, local copies, waits for them, and re-layouts: 102 us -> 0.62 us
    all_to_all x8 -> x0, waiting for transfers between devices: 89.9 us -> none  [the longest x1 28.5 us: local_step(): lax.all_to_all(o_all.reshape(seq_len, q_loc, HEAD_DIM), 'sp', 0, 1, tiled...]
  transfers between devices with their start and end apart: 9 -> 6, of which waited for: 7 -> 6; matrix products, arithmetic and copies ran while one was open for 19% -> 15% of each run, Pallas kernels for 0% -> 8%
where the time goes in v1:
time: 930 us; the launch traced here: 921 us
  waiting for transfers between devices  350 us (38%)
  matrix products  320 us (34%)
  Pallas kernels  163 us (18%)
  blocking collectives  36.6 us (4%)
  other arithmetic  31.7 us (3%)
  between operations  14.6 us (2%)
    all_gather x6, waiting for transfers between devices, gather(): return lax.all_gather(val, 'sp', axis=0, tiled=True)  348 us
    dot_general x9, matrix products, dot(): return lax.dot_general(a, b, dims, preferred_element_type=F32)  320 us
    pallas_call x1, Pallas kernels, attn_backward(): pl.pallas_call(functools.partial(attn_bwd_kernel, heads), grid=(n_blocks,...  86.5 us
    pallas_call x1, Pallas kernels, attn_forward(): pl.pallas_call(functools.partial(attn_fwd_kernel, heads), grid=(n_blocks,...  49.9 us
    pallas_call x1, Pallas kernels, project(): pl.pallas_call(functools.partial(project_kernel, heads), grid=(seq_len //...  26.2 us
    psum x1, blocking collectives, local_step(): grad_gain = lax.psum(jnp.sum(d_hidden * normed, axis=0), 'sp')  25.9 us
  transfers between devices with their start and end apart: 6, of which 6 were waited for; matrix products, arithmetic and copies ran while one was open for 15% of the time, Pallas kernels for 8%

profile of v1, /device:TPU:0, one launch (start us, length us, event | category | flops | bytes accessed | tf_op | source)
XLA Modules:
  0.0 920.8 jit_solution(8667999979618906435)
XLA Ops:
  7.2 0.0 all-gather.8.cloned.1.call-start
  7.2 2.6 fusion.11
  9.8 0.7 convert_element_type.36
  10.5 0.0 copy-done.3
  10.5 0.6 copy-done.1
  11.1 4.7 fusion.4
  15.9 0.0 all-gather.8.cloned.1.call-update
  15.9 0.0 all-gather.12.cloned.1.call-start
  15.9 0.7 all-gather.12.cloned.1.call-update
  16.6 0.0 all-gather.18.cloned.1.call-start
  16.7 0.0 copy-done.5
  16.7 10.6 %all-gather = s32[8,1,512]{2,1,0:T(1,128)S(1)} all-gather(s32[1,1,512]{2,1,0:T(1,128)S(1)} %bitcast.22), channel_id=1, replica_groups=mesh['dp'=2,'sp'=8] {'sp'}, dimensions={0}, use_global_device_ids=true | all-gather | bytes 18432 | tf_op jit(solution)/shard_map/all_gather | solution.py:228
  27.4 4.8 multiply_sine_fusion.1
  32.2 1.5 constant_dynamic-slice_fusion
  33.7 1.9 constant_dynamic-slice_fusion.2
  35.6 2.1 pad_maximum_fusion.w_ref
  37.8 7.5 fusion.21
  45.2 3.2 pad_maximum_fusion.1
  48.4 91.9 %all-gather.8.cloned.1.call-done.h_ref = bf16[4096,3072]{1,0:T(8,128)(2,1)} async-done(((bf16[512,3072]{1,0:T(8,128)(2,1)}), bf16[4096,3072]{1,0:T(8,128)(2,1)}) %all-gather.8.cloned.1.call-update) | async-done | bytes 25165840 | tf_op jit(solution)/shard_map/all_gather | solution.py:228
  140.3 26.2 %project.1 = (bf16[4096,384]{1,0:T(8,128)(2,1)}, bf16[4096,128]{1,0:T(8,128)(2,1)}, bf16[4096,128]{1,0:T(8,128)(2,1)}) custom-call(bf16[4096,3072]{1,0:T(8,128)(2,1)} %all-gather.8.cloned.1.call-done.h_ref, bf16[3072,640]{1,0:T(8,128)(2,1)} %pad_maximum_fusion.w_ref, f32[4096,128]{1,0:T(8,128)} %get-tuple-element.33.cos_ref, ...), custom_call_target="tpu_custom_call" | custom-call | flops 16106127360 | bytes 25165824 | tf_op jit(solution)/shard_map/project/pallas_call | solution.py:57
  166.5 49.9 %attn_fwd.1 = (bf16[384,4096]{1,0:T(8,128)(2,1)}, f32[8,4096]{1,0:T(8,128)}) custom-call(bf16[4096,384]{1,0:T(8,128)(2,1)} %get-tuple-element.15.q_ref, bf16[4096,128]{1,0:T(8,128)(2,1)} %get-tuple-element.16.k_ref, bf16[4096,128]{1,0:T(8,128)(2,1)} %get-tuple-element.17.v_ref), custom_call_target="tpu_custom_call" | custom-call | flops 28991029248 | bytes 6291456 | tf_op jit(solution)/shard_map/attn_fwd/pallas_call | solution.py:120
  216.5 47.1 %all-gather.12.cloned.1.call-done = bf16[4096,3072]{1,0:T(8,128)(2,1)} async-done(((bf16[512,3072]{1,0:T(8,128)(2,1)}), bf16[4096,3072]{1,0:T(8,128)(2,1)}) %all-gather.12.cloned.1.call-update) | async-done | bytes 25165840 | tf_op jit(solution)/shard_map/all_gather | solution.py:228
  263.6 20.0 %fusion.13.do_ref = bf16[4096,384]{1,0:T(8,128)(2,1)} fusion(bf16[4096,3072]{1,0:T(8,128)(2,1)} %all-gather.12.cloned.1.call-done, bf16[3072,3072]{1,0:T(8,128)(2,1)} %param.15, s32[]{:T(128)S(6)} %select_n.6), kind=kOutput, calls=%fused_computation.18 | convolution fusion | flops 9665249280 | bytes 30670852 | tf_op jit(solution)/shard_map/dot_general | solution.py:27
  283.6 86.5 %attn_bwd.1 = (bf16[384,4096]{1,0:T(8,128)(2,1)}, bf16[128,4096]{1,0:T(8,128)(2,1)}, bf16[128,4096]{1,0:T(8,128)(2,1)}) custom-call(bf16[4096,384]{1,0:T(8,128)(2,1)} %get-tuple-element.15.q_ref, bf16[4096,128]{1,0:T(8,128)(2,1)} %get-tuple-element.16.k_ref, bf16[4096,128]{1,0:T(8,128)(2,1)} %get-tuple-element.17.v_ref, bf16[4096,384]{1,0:T(8,128)(2,1)} %fusion.13.do_ref, ...), custom_call_target="tpu_custom_call" | custom-call | flops 72477573120 | bytes 12582912 | tf_op jit(solution)/shard_map/attn_bwd/pallas_call | solution.py:205
  370.1 0.0 all-gather.18.cloned.1.call-update
  370.2 0.0 all-gather.16.cloned.1.call-start
  370.2 0.5 all-gather.16.cloned.1.call-update
  370.7 0.0 all-gather.14.cloned.1.call-start
  370.8 0.5 all-gather.14.cloned.1.call-update
  371.3 0.4 all-gather.10.cloned.1.call-start
  371.8 0.1 all-gather.10.cloned.1.call-update
  371.9 48.9 %all-gather.18.cloned.1.call-done = bf16[1024,4096]{1,0:T(8,128)(2,1)} async-done(((bf16[128,4096]{1,0:T(8,128)(2,1)}), bf16[1024,4096]{1,0:T(8,128)(2,1)}) %all-gather.18.cloned.1.call-update) | async-done | bytes 8388624 | tf_op jit(solution)/shard_map/all_gather | solution.py:228
  420.8 9.5 %fusion.17 = f32[512,3072]{1,0:T(8,128)} fusion(bf16[3072,1024]{1,0:T(8,128)(2,1)} %param.14, bf16[1024,4096]{1,0:T(8,128)(2,1)} %all-gather.18.cloned.1.call-done, s32[]{:T(128)S(6)} %select_n.16), kind=kOutput, calls=%fused_computation.29 | convolution fusion | flops 3221225472 | bytes 13631492 | tf_op jit(solution)/shard_map/dot_general | solution.py:27
  430.3 43.3 %all-gather.16.cloned.1.call-done = bf16[1024,4096]{1,0:T(8,128)(2,1)} async-done(((bf16[128,4096]{1,0:T(8,128)(2,1)}), bf16[1024,4096]{1,0:T(8,128)(2,1)}) %all-gather.16.cloned.1.call-update) | async-done | bytes 8388624 | tf_op jit(solution)/shard_map/all_gather | solution.py:228
  473.6 10.2 %fusion.19 = f32[512,3072]{1,0:T(8,128)} fusion(bf16[3072,1024]{1,0:T(8,128)(2,1)} %param.13, bf16[1024,4096]{1,0:T(8,128)(2,1)} %all-gather.16.cloned.1.call-done, s32[]{:T(128)S(6)} %select_n.16), kind=kOutput, calls=%fused_computation.31 | convolution fusion | flops 3221225472 | bytes 13631492 | tf_op jit(solution)/shard_map/dot_general | solution.py:27
  483.8 0.0 copy-done.6
  483.8 32.5 %fusion.29 = f32[3072,1024]{1,0:T(8,128)} fusion(bf16[4096,3072]{1,0:T(8,128)(2,1)} %all-gather.8.cloned.1.call-done.h_ref, bf16[1024,4096]{1,0:T(8,128)(2,1)S(1)} %copy-done.6), kind=kOutput, calls=%fused_computation.48 | convolution fusion | flops 25769803776 | bytes 46137344 | tf_op jit(solution)/shard_map/dot_general | solution.py:27
  516.3 34.0 %fusion.28 = f32[3072,1024]{1,0:T(8,128)} fusion(bf16[4096,3072]{1,0:T(8,128)(2,1)} %all-gather.8.cloned.1.call-done.h_ref, bf16[1024,4096]{1,0:T(8,128)(2,1)} %all-gather.16.cloned.1.call-done), kind=kOutput, calls=%fused_computation.47 | convolution fusion | flops 25769803776 | bytes 46137344 | tf_op jit(solution)/shard_map/dot_general | solution.py:27
  550.3 46.5 %all-gather.14.cloned.1.call-done = bf16[3072,4096]{1,0:T(8,128)(2,1)} async-done(((bf16[384,4096]{1,0:T(8,128)(2,1)}), bf16[3072,4096]{1,0:T(8,128)(2,1)}) %all-gather.14.cloned.1.call-update) | async-done | bytes 25165840 | tf_op jit(solution)/shard_map/all_gather | solution.py:228
  596.8 0.0 copy-done
  596.8 0.0 copy-done.4
  596.8 21.3 %fusion.10 = (f32[3072]{0:T(1024)S(1)}, f32[512]{0:T(512)S(1)}, f32[512,3072]{1,0:T(8,128)}) fusion(bf16[512,3072]{1,0:T(8,128)(2,1)S(1)} %copy-done, f32[512]{0:T(512)S(1)} %copy-done.4, f32[3072]{0:T(1024)S(1)} %copy-done.2, f32[512,3072]{1,0:T(8,128)} %fusion.17, f32[512,3072]{1,0:T(8,128)} %fusion.19, bf16[3072,3072]{1,0:T(8,128)(2,1)} %param.12, ...), kind=kOutput, calls=%fused_computation.13 | convolution fusion | flops 9677828096 | bytes 44068868 | tf_op jit(solution)/shard_map/dot_general | solution.py:27
  618.1 25.9 %psum.7 = f32[3072]{0:T(1024)} all-reduce(f32[3072]{0:T(1024)S(1)} %get-tuple-element.23), channel_id=1, replica_groups=mesh['dp'=2,'sp'=8] {'sp'}, use_global_device_ids=true, to_apply=%region_3.0 | all-reduce | flops 3072 | bytes 24576 | tf_op jit(solution)/shard_map/psum | solution.py:263
  644.1 6.1 fusion.9
  650.1 70.7 %all-gather.10.cloned.1.call-done = bf16[3072,4096]{1,0:T(8,128)(2,1)} async-done(((bf16[384,4096]{1,0:T(8,128)(2,1)}), bf16[3072,4096]{1,0:T(8,128)(2,1)}) %all-gather.10.cloned.1.call-update) | async-done | bytes 25165840 | tf_op jit(solution)/shard_map/all_gather | solution.py:228
  720.8 16.0 %fusion.12 = bf16[512,3072]{1,0:T(8,128)(2,1)} fusion(bf16[512,3072]{1,0:T(8,128)(2,1)S(1)} %copy-done, bf16[3072,3072]{1,0:T(8,128)(2,1)} %param.15, bf16[3072,4096]{1,0:T(8,128)(2,1)} %all-gather.10.cloned.1.call-done, s32[]{:T(128)S(6)} %select_n.16), kind=kOutput, calls=%fused_computation.15 | convolution fusion | flops 9668395008 | bytes 28311556 | tf_op jit(solution)/shard_map/dot_general | solution.py:27
  736.8 87.1 %fusion.30 = f32[3072,3072]{1,0:T(8,128)} fusion(bf16[3072,4096]{1,0:T(8,128)(2,1)} %all-gather.10.cloned.1.call-done, bf16[4096,3072]{1,0:T(8,128)(2,1)} %all-gather.12.cloned.1.call-done), kind=kOutput, calls=%fused_computation.49 | convolution fusion | flops 77309411328 | bytes 88080384 | tf_op jit(solution)/shard_map/dot_general | solution.py:27
  823.9 89.6 %fusion.27 = f32[3072,3072]{1,0:T(8,128)} fusion(bf16[4096,3072]{1,0:T(8,128)(2,1)} %all-gather.8.cloned.1.call-done.h_ref, bf16[3072,4096]{1,0:T(8,128)(2,1)} %all-gather.14.cloned.1.call-done), kind=kOutput, calls=%fused_computation.46 | convolution fusion | flops 77309411328 | bytes 88080384 | tf_op jit(solution)/shard_map/dot_general | solution.py:27
  (13 shorter events, 0.0 us)
Async XLA Ops:
  7.2 133.1 %all-gather.8.cloned.1.call-start = ((), (), s32[]{:S(2)}) async-start(), calls=%async_computation | async-start | bytes 28311552 | tf_op jit(solution)/shard_map/all_gather | solution.py:228
  9.8 0.7 copy-start.3
  10.5 0.6 copy-start.1
  11.1 5.6 copy-start.5
  15.9 247.7 %all-gather.12.cloned.1.call-start = ((), (), s32[]{:S(2)}) async-start(), calls=%async_computation.2 | async-start | bytes 28311552 | tf_op jit(solution)/shard_map/all_gather | solution.py:228
  16.6 404.2 %all-gather.18.cloned.1.call-start = ((), (), s32[]{:S(2)}) async-start(), calls=%async_computation.5 | async-start | bytes 9437184 | tf_op jit(solution)/shard_map/all_gather | solution.py:228
  370.2 103.5 %all-gather.16.cloned.1.call-start = ((), (), s32[]{:S(2)}) async-start(), calls=%async_computation.4 | async-start | bytes 9437184 | tf_op jit(solution)/shard_map/all_gather | solution.py:228
  370.7 226.1 %all-gather.14.cloned.1.call-start = ((), (), s32[]{:S(2)}) async-start(), calls=%async_computation.3 | async-start | bytes 28311552 | tf_op jit(solution)/shard_map/all_gather | solution.py:228
  371.3 349.5 %all-gather.10.cloned.1.call-start = ((), (), s32[]{:S(2)}) async-start(), calls=%async_computation.1 | async-start | bytes 28311552 | tf_op jit(solution)/shard_map/all_gather | solution.py:228
  473.6 10.2 %copy-start.6 = (bf16[1024,4096]{1,0:T(8,128)(2,1)S(1)}, bf16[1024,4096]{1,0:T(8,128)(2,1)}, u32[]{:S(2)}) copy-start(bf16[1024,4096]{1,0:T(8,128)(2,1)} %all-gather.18.cloned.1.call-done) | copy-start | bytes 25165828
  516.3 80.5 %copy-start = (bf16[512,3072]{1,0:T(8,128)(2,1)S(1)}, bf16[512,3072]{1,0:T(8,128)(2,1)}, u32[]{:S(2)}) copy-start(bf16[512,3072]{1,0:T(8,128)(2,1)} %param.8) | copy-start | bytes 9437188
  516.3 80.5 %copy-start.2 = (f32[3072]{0:T(1024)S(1)}, f32[3072]{0:T(1024)}, u32[]{:S(2)}) copy-start(f32[3072]{0:T(1024)} %copy-done.1) | copy-start | bytes 36868
  516.3 80.5 %copy-start.4 = (f32[512]{0:T(512)S(1)}, f32[512]{0:T(512)}, u32[]{:S(2)}) copy-start(f32[512]{0:T(512)} %copy-done.3) | copy-start | bytes 6148
Sparse Core Ops, SparseCore 0:
  16.0 124.2 all-gather.7
  142.1 121.4 all-gather.11
  370.3 50.4 all-gather.17
  423.1 50.4 all-gather.15
  475.3 121.4 all-gather.13
  599.1 121.6 all-gather.9
